TPU v7x, 32 devices: a whole 2x2x4 slice. The times are simulated.
32 devices in a mesh: groups: 2 (over x), seq: 8 (over z, y), expert: 2 (over core).
Axes of the slice: x: 2, y: 2, z: 4, core: 2. Of those that a mesh axis runs over, the one named last changes fastest.
Arguments:
- residual: bfloat16 [8, 6144], P('groups', 'seq'), parts along dimension 0, may hold values from -27 to 27
- queries: bfloat16 [8, 6144], P('groups', 'expert'), parts along dimension 0, may hold values from -6 to 6
- new_entries: bfloat16 [2, 8, 1024], P(None, 'groups', 'expert'), parts along dimension 1, may hold values from -6 to 6
- kv_cache: bfloat16 [2, 1024, 16384], P(None, 'seq', ('groups', 'expert')), parts along dimension 2, may hold values from -6 to 6
- lengths: int32 [8], P('groups'), parts along dimension 0, may hold values from 128 to 2048, as said below
- routing: int32 [8, 2], P('groups'), parts along dimension 0, may hold values from 0 to 3, all different within a row
- w_out: bfloat16 [6144, 6144], P('expert', 'seq'), may hold values from -0.5 to 0.5
- norm_gain: bfloat16 [6144], replicated, may hold values from 0.5 to 1.5
- router: bfloat16 [6144, 4], replicated, may hold values from -0.078125 to 0.078125
- w_gate: bfloat16 [4, 6144, 1024], P('expert', None, 'seq'), may hold values from -0.078125 to 0.078125
- w_up: bfloat16 [4, 6144, 1024], P('expert', None, 'seq'), may hold values from -0.078125 to 0.078125
- w_down: bfloat16 [4, 1024, 6144], P('expert', 'seq'), may hold values from -0.75 to 0.75
Outputs:
- attended: bfloat16 [8, 6144], P('groups', 'seq'), parts along dimension 0
- expert_out: bfloat16 [8, 6144], P('groups', 'seq'), parts along dimension 0
There are 2 independent parts, one for each index of `groups`. A program takes and returns all parts, laid end to end along the dimension named above; an argument that names none is the same for every part. Nothing has to cross between parts.
Inputs may be any that keep to these rules, and one draw needn't show every extreme that they name: `lengths`: every draw has a request of exactly 2048 positions. `routing`: each request names two different experts.
All inputs are finite; a program needn't handle non-finite values.
Results may differ from a plain program's by a relative error of at most 0.02.
Values may be sent and summed in bfloat16 or wider, within the bound.
A program may use at most 128 MiB of HBM per device.

v0:
```python
import math

import jax
import jax.numpy as jnp
from jax import lax
from jax.sharding import PartitionSpec as P

H = 48
KVH = 8
HD = 128


def combined_all(value, axis, join):
    pieces = jax.tree.map(lambda part: lax.all_gather(part, axis), value)
    head = jax.tree.map(lambda part: part[0], pieces)
    tail = jax.tree.map(lambda part: part[1:], pieces)
    running, _ = lax.scan(lambda running, share: (join(running, share), None), head, tail)
    return running


def merge_parts(earlier, later):
    high_left, total_left, sum_left = earlier
    high_right, total_right, sum_right = later
    joined = jnp.maximum(high_left, high_right)
    scale_left = jnp.exp(high_left - joined)
    scale_right = jnp.exp(high_right - joined)
    return (
        joined,
        total_left * scale_left + total_right * scale_right,
        sum_left * scale_left[..., None] + sum_right * scale_right[..., None],
    )


def partial_attention(query_rows, relaid, positions, lengths, kv_count):
    requests = lengths.shape[0]
    per_group = H // KVH
    slot_count = relaid.shape[2] // requests
    query_heads = query_rows.reshape(requests, kv_count, per_group, HD)
    key_rows = relaid[0].reshape(kv_count, HD, slot_count, requests)
    value_rows = relaid[1].reshape(kv_count, HD, slot_count, requests)
    scores = jnp.einsum(
        "rgtd,gdpr->rgtp", query_heads, key_rows, preferred_element_type=jnp.float32
    ) * (1.0 / math.sqrt(HD))
    alive_mask = (positions[None, :] < lengths[:, None])[:, None, None, :]
    highest = jnp.max(jnp.where(alive_mask, scores, -1e30), axis=-1)
    weights = jnp.where(alive_mask, jnp.exp(scores - highest[..., None]), 0.0)
    summed = jnp.einsum(
        "rgtp,gdpr->rgtd",
        weights.astype(jnp.bfloat16),
        value_rows,
        preferred_element_type=jnp.float32,
    )
    return (highest, jnp.sum(weights, axis=-1), summed)


def on_device(
    residual,
    queries,
    new_entries,
    kv_cache,
    lengths,
    routing,
    w_out,
    norm_gain,
    router,
    w_gate,
    w_up,
    w_down,
):
    requests = lengths.shape[0]
    seq_count = lax.axis_size("seq")
    core_count = lax.axis_size("expert")
    seq_index = lax.axis_index("seq")
    core_index = lax.axis_index("expert")
    half_ctx = kv_cache.shape[2] // requests
    ctx_dev = half_ctx // seq_count
    own_heads = KVH // core_count
    relaid = lax.all_to_all(kv_cache, "seq", split_axis=2, concat_axis=1, tiled=True)
    positions = core_index * half_ctx + seq_index * ctx_dev + jnp.arange(ctx_dev, dtype=jnp.int32)
    all_queries = lax.all_gather(queries, "expert", axis=1, tiled=True)
    partials = partial_attention(all_queries, relaid, positions, lengths, KVH)
    merged = combined_all(partials, ("seq", "expert"), merge_parts)
    head_start = core_index * own_heads
    highest = lax.dynamic_slice_in_dim(merged[0], head_start, own_heads, 1)
    totals = lax.dynamic_slice_in_dim(merged[1], head_start, own_heads, 1)
    summed = lax.dynamic_slice_in_dim(merged[2], head_start, own_heads, 1)
    per_group = H // KVH
    query_heads = queries.reshape(requests, own_heads, per_group, HD)
    new_keys = new_entries[0].reshape(requests, own_heads, HD)
    new_values = new_entries[1].reshape(requests, own_heads, HD).astype(jnp.float32)
    own_score = jnp.einsum(
        "rgtd,rgd->rgt", query_heads, new_keys, preferred_element_type=jnp.float32
    ) * (1.0 / math.sqrt(HD))
    joined = jnp.maximum(highest, own_score)
    fade_old = jnp.exp(highest - joined)
    own_weight = jnp.exp(own_score - joined)
    numerator = summed * fade_old[..., None] + own_weight[..., None] * new_values[:, :, None, :]
    denominator = totals * fade_old + own_weight
    attn_rows = (
        (numerator / denominator[..., None])
        .reshape(requests, own_heads * per_group * HD)
        .astype(jnp.bfloat16)
    )
    head_terms = jnp.dot(attn_rows, w_out, preferred_element_type=jnp.float32)
    attended = (residual.astype(jnp.float32) + lax.psum(head_terms, "expert")).astype(jnp.bfloat16)
    gathered = lax.all_gather(attended, "seq", axis=1, tiled=True)
    widened = gathered.astype(jnp.float32)
    mean_square = jnp.mean(widened * widened, axis=-1, keepdims=True)
    normed = (widened * lax.rsqrt(mean_square + 1e-05) * norm_gain.astype(jnp.float32)).astype(
        jnp.bfloat16
    )
    logits = jnp.dot(normed, router, preferred_element_type=jnp.float32)
    expert_total = router.shape[1]
    picked = (
        routing[:, :, None] == jnp.arange(expert_total, dtype=jnp.int32)[None, None, :]
    ).astype(jnp.float32)
    chosen = jnp.sum(picked * logits[:, None, :], axis=-1)
    first_share = jax.nn.sigmoid(chosen[:, 0] - chosen[:, 1])
    shares = jnp.stack([first_share, 1.0 - first_share], axis=-1)
    combine = jnp.sum(picked * shares[:, :, None], axis=1)
    local_ids = core_index * w_gate.shape[0] + jnp.arange(w_gate.shape[0], dtype=jnp.int32)
    select = (jnp.arange(expert_total, dtype=jnp.int32)[:, None] == local_ids[None, :]).astype(
        jnp.float32
    )
    local_share = jnp.sum(combine[:, :, None] * select[None, :, :], axis=1)
    gate_proj = jnp.einsum("rd,edf->ref", normed, w_gate, preferred_element_type=jnp.float32)
    upward = jnp.einsum("rd,edf->ref", normed, w_up, preferred_element_type=jnp.float32)
    activation = (jax.nn.silu(gate_proj) * upward * local_share[:, :, None]).astype(jnp.bfloat16)
    expert_terms = jnp.einsum("ref,efd->rd", activation, w_down, preferred_element_type=jnp.float32)
    reduced = lax.psum_scatter(expert_terms, "seq", scatter_dimension=1, tiled=True)
    expert_out = lax.psum(reduced, "expert").astype(jnp.bfloat16)
    return (attended, expert_out)


def solution(mesh):
    in_specs = (
        P("groups", "seq"),
        P("groups", "expert"),
        P(None, "groups", "expert"),
        P(None, "seq", ("groups", "expert")),
        P("groups"),
        P("groups", None),
        P("expert", "seq"),
        P(),
        P(),
        P("expert", None, "seq"),
        P("expert", None, "seq"),
        P("expert", "seq", None),
    )
    out_specs = (P("groups", "seq"), P("groups", "seq"))
    return jax.shard_map(
        on_device, mesh=mesh, in_specs=in_specs, out_specs=out_specs, check_vma=False
    )
```

profile of v0, /device:TPU:0, one launch (start us, length us, event | category | flops | bytes accessed | tf_op | source)
XLA Modules:
  0.0 286.1 jit_solution(10244432440107724800)
XLA Ops:
  7.2 6.3 %copy.89 = bf16[2,128,4096]{1,0,2:T(2,128)(2,1)} copy(bf16[2,128,4096]{2,1,0:T(8,128)(2,1)} %param.17) | data formatting | bytes 4194304 | tf_op args[3]
  13.5 7.4 %all-to-all-start = ((bf16[2,128,4096]{1,0,2:T(2,128)(2,1)}), bf16[2,128,4096]{1,0,2:T(2,128)(2,1)}, u32[]{:S(2)}, u32[]{:S(2)}) async-start(bf16[2,128,4096]{1,0,2:T(2,128)(2,1)} %copy.89), calls=%async_computation | async-start | bytes 4194304 | tf_op jit(solution)/shard_map/all_to_all | solution.py:78
  21.0 1.8 all_gather.24
  23.0 46.3 %all-to-all-done = bf16[2,128,4096]{1,0,2:T(2,128)(2,1)} async-done(((bf16[2,128,4096]{1,0,2:T(2,128)(2,1)}), bf16[2,128,4096]{1,0,2:T(2,128)(2,1)}, u32[]{:S(2)}, u32[]{:S(2)}) %all-to-all-start) | async-done | bytes 2097184 | tf_op jit(solution)/shard_map/all_to_all | solution.py:78
  69.3 1.9 copy.90
  71.2 0.2 fusion.34
  71.4 0.7 select_reduce_fusion
  72.1 0.4 fusion.6
  72.6 0.7 copy.95
  73.4 0.6 reshape.97
  74.0 0.6 compare_convert_fusion
  74.6 0.7 fusion.35
  75.4 0.2 fusion.10
  75.6 20.3 %all-gather.1 = f32[64,8,6]{2,1,0:T(8,128)S(1)} all-gather(f32[4,8,6]{2,1,0:T(8,128)S(1)} %fusion.10), channel_id=3, replica_groups=mesh['groups'=2,'seq'=8,'expert'=2] {'seq','expert'}, dimensions={0}, use_global_device_ids=true | all-gather | bytes 13056 | tf_op jit(solution)/shard_map/all_gather | solution.py:14
  95.9 18.6 %all-gather = f32[64,8,6]{2,1,0:T(8,128)S(1)} all-gather(f32[4,8,6]{2,1,0:T(8,128)S(1)} %get-tuple-element.106), channel_id=2, replica_groups=mesh['groups'=2,'seq'=8,'expert'=2] {'seq','expert'}, dimensions={0}, use_global_device_ids=true | all-gather | bytes 13056 | tf_op jit(solution)/shard_map/all_gather | solution.py:14
  114.5 0.7 slice.61
  115.2 0.6 slice.57
  115.8 1.1 copy.102
  117.0 1.4 copy.101
  118.4 0.8 copy.98
  119.2 0.9 slice.60
  120.2 2.6 slice.63
  122.7 30.3 %while.14 = (s32[]{:T(128)}, f32[4,8,6]{1,0,2:T(4,128)S(1)}, f32[4,8,6]{1,0,2:T(4,128)S(1)}, f32[4,8,6,128]{3,2,1,0:T(8,128)S(1)}, f32[15,4,8,6]{2,1,3,0:T(4,128...) while((s32[]{:T(128)}, f32[4,8,6]{1,0,2:T(4,128)S(1)}, ...), condition=%wide.region_3.4_spmd, body=%wide.region_2.3_spmd.sunk | while | flops 74882 | bytes 502365 | solution.py:17
  122.7 0.7 fusion.50
  123.7 0.9 constant_dynamic-slice_fusion.2
  124.8 0.7 fusion.50
  125.7 0.9 constant_dynamic-slice_fusion.2
  126.8 0.7 fusion.50
  127.7 0.9 constant_dynamic-slice_fusion.2
  128.8 0.7 fusion.50
  129.8 0.9 constant_dynamic-slice_fusion.2
  130.8 0.7 fusion.50
  131.8 0.9 constant_dynamic-slice_fusion.2
  132.9 0.7 fusion.50
  133.8 0.9 constant_dynamic-slice_fusion.2
  134.9 0.7 fusion.50
  135.8 0.9 constant_dynamic-slice_fusion.2
  136.9 0.7 fusion.50
  137.9 0.9 constant_dynamic-slice_fusion.2
  138.9 0.7 fusion.50
  139.9 0.9 constant_dynamic-slice_fusion.2
  141.0 0.7 fusion.50
  141.9 0.9 constant_dynamic-slice_fusion.2
  143.0 0.7 fusion.50
  143.9 0.9 constant_dynamic-slice_fusion.2
  145.0 0.7 fusion.50
  145.9 0.9 constant_dynamic-slice_fusion.2
  147.0 0.7 fusion.50
  148.0 0.9 constant_dynamic-slice_fusion.2
  149.0 0.7 fusion.50
  150.0 0.9 constant_dynamic-slice_fusion.2
  151.1 0.7 fusion.50
  152.0 0.9 constant_dynamic-slice_fusion.2
  153.3 0.7 multiply_add_fusion
  154.0 0.8 divide_convert_fusion
  154.9 3.1 %fusion.36 = f32[4,768]{1,0:T(4,128)S(1)} fusion(bf16[4,3072]{1,0:T(4,128)(2,1)S(1)} %convert_element_type.53, bf16[3072,768]{1,0:T(8,128)(2,1)} %param.20), kind=kOutput, calls=%fused_computation.63 | convolution fusion | flops 18874368 | bytes 4755456 | tf_op jit(solution)/shard_map/dot_general | solution.py:104
  158.0 3.5 %psum.14 = f32[4,768]{1,0:T(4,128)S(1)} all-reduce(f32[4,768]{1,0:T(4,128)S(1)} %fusion.36), channel_id=1, replica_groups=mesh['groups'=2,'seq'=8,'expert'=2] {'expert'}, use_global_device_ids=true, to_apply=%region_4.5 | all-reduce | flops 3072 | bytes 24576 | tf_op jit(solution)/shard_map/psum | solution.py:105
  161.5 30.8 %all_gather.31 = bf16[4,6144]{1,0:T(4,128)(2,1)S(1)} all-gather(bf16[4,768]{1,0:T(4,128)(2,1)S(1)} %add_convert_fusion), channel_id=1, replica_groups=mesh['groups'=2,'seq'=8,'expert'=2] {'seq'}, dimensions={1}, use_global_device_ids=true | all-gather | bytes 55296 | tf_op jit(solution)/shard_map/all_gather | solution.py:106
  192.2 0.2 fusion.11
  193.0 2.4 fusion.20
  195.5 5.8 %convolution_bitcast_fusion = f32[6144,4]{1,0:T(8,128)} fusion(bf16[2,128,6144]{2,1,0:T(8,128)(2,1)S(1)} %copy-done, bf16[2,6144,128]{2,1,0:T(8,128)(2,1)} %param.24, bf16[4,6144]{1,0:T(4,128)(2,1)S(1)} %fusion.13, f32[4,2,128]{2,0,1:T(4,128)S(1)} %fusion.20, f32[4,2]{0,1:T(2,128)S(1)} %multiply_reduce_fusion), kind=kOutput, calls=%fused_computation.10 | convolution fusion | flops 25172992 | bytes 6443040 | tf_op jit(solution)/shard_map/ref,efd->rd/dot_general | solution.py:129
  201.3 72.9 %reduce-scatter.4.cloned.1.call-done = f32[768,4]{1,0:T(8,128)} async-done(((f32[6144,4]{1,0:T(8,128)}), f32[768,4]{1,0:T(8,128)}) %reduce-scatter.4.cloned.1.call-update) | async-done | bytes 12304
  274.2 1.1 copy.117
  275.4 3.9 %psum.15 = bf16[4,768]{1,0:T(4,128)(2,1)} all-reduce(f32[4,768]{1,0:T(4,128)S(1)} %copy.117), channel_id=1, replica_groups=mesh['groups'=2,'seq'=8,'expert'=2] {'expert'}, use_global_device_ids=true, to_apply=%region_10.11 | all-reduce | flops 3072 | bytes 18432 | tf_op jit(solution)/shard_map/psum | solution.py:131
  (94 shorter events, 6.7 us)
Async XLA Ops:
  7.2 188.3 %copy-start = (bf16[2,128,6144]{2,1,0:T(8,128)(2,1)S(1)}, bf16[2,128,6144]{2,1,0:T(8,128)(2,1)}, u32[]{:S(2)}) copy-start(bf16[2,128,6144]{2,1,0:T(8,128)(2,1)} %param.25) | copy-start | bytes 9437188
  13.5 7.5 %copy-start.1 = (bf16[4,3072]{1,0:T(4,128)(2,1)S(1)}, bf16[4,3072]{1,0:T(4,128)(2,1)}, u32[]{:S(2)}) copy-start(bf16[4,3072]{1,0:T(4,128)(2,1)} %param.15) | copy-start | bytes 73732
  13.5 9.4 %copy-start.9 = (s32[4]{0:T(128)S(1)}, s32[4]{0:T(128)}, u32[]{:S(2)}) copy-start(s32[4]{0:T(128)} %param.18) | copy-start | bytes 52
  13.5 55.8 %all-to-all-start = ((bf16[2,128,4096]{1,0,2:T(2,128)(2,1)}), bf16[2,128,4096]{1,0,2:T(2,128)(2,1)}, u32[]{:S(2)}, u32[]{:S(2)}) async-start(bf16[2,128,4096]{1,0,2:T(2,128)(2,1)} %copy.89), calls=%async_computation | async-start | bytes 4194304 | tf_op jit(solution)/shard_map/all_to_all | solution.py:78
  21.0 98.3 %all-gather.5.cloned.1.call-start = ((), (), s32[]{:S(2)}) async-start(), calls=%async_computation.2 | async-start | bytes 1671168 | tf_op jit(solution)/shard_map/all_gather | solution.py:14
  71.2 2.2 copy-start.4
  71.2 2.8 copy-start.3
  73.3 201.0 %reduce-scatter.4.cloned.1.call-start = ((), (), s32[]{:S(2)}) async-start(), calls=%async_computation.3 | async-start | bytes 3538944
  153.1 8.3 %copy-start.5 = (bf16[4,768]{1,0:T(4,128)(2,1)S(1)}, bf16[4,768]{1,0:T(4,128)(2,1)}, u32[]{:S(2)}) copy-start(bf16[4,768]{1,0:T(4,128)(2,1)} %param.14) | copy-start | bytes 18436
  153.1 39.4 %copy-start.8 = (bf16[6144,4]{0,1:T(4,128)(2,1)S(1)}, bf16[6144,4]{0,1:T(4,128)(2,1)}, u32[]{:S(2)}) copy-start(bf16[6144,4]{0,1:T(4,128)(2,1)} %param.22) | copy-start | bytes 147460
  153.1 39.6 %copy-start.6 = (s32[4,2]{0,1:T(2,128)S(1)}, s32[4,2]{0,1:T(2,128)}, u32[]{:S(2)}) copy-start(s32[4,2]{0,1:T(2,128)} %param.19) | copy-start | bytes 100
  154.9 40.5 %copy-start.7 = (f32[4,2]{0,1:T(2,128)S(1)}, f32[4,2]{0,1:T(2,128)}, u32[]{:S(2)}) copy-start(f32[4,2]{0,1:T(2,128)} %compare_convert_fusion) | copy-start | bytes 100
  161.4 39.9 %copy-start.2 = (bf16[4,768]{1,0:T(4,128)(2,1)}, bf16[4,768]{1,0:T(4,128)(2,1)S(1)}, u32[]{:S(2)}) copy-start(bf16[4,768]{1,0:T(4,128)(2,1)S(1)} %add_convert_fusion) | copy-start | bytes 18436
Sparse Core Ops, SparseCore 0:
  73.4 39.7 all-gather.4
  201.5 72.7 reduce-scatter.3
where the time goes:
time: 288 us; the launch traced here: 286 us
  waiting for transfers between devices  119 us (41%)
  blocking collectives  78.8 us (27%)
  local copies, waits for them, and re-layouts  35.9 us (12%)
  other arithmetic  16.7 us (6%)
  between operations  14.3 us (5%)
  matrix products  13.4 us (5%)
  starting transfers between devices  7.52 us (3%)
    unnamed x3, waiting for transfers between devices  72.9 us
    all_to_all x1, waiting for transfers between devices, on_device(): lax.all_to_all(kv_cache, 'seq', split_axis=2, concat_axis=1, tiled=True)  46.3 us
    all_gather x2, blocking collectives, combined_all(): pieces = jax.tree.map(lambda part: lax.all_gather(part, axis), value)  38.9 us
    all_gather x1, blocking collectives, on_device(): gathered = lax.all_gather(attended, 'seq', axis=1, tiled=True)  30.8 us
    dynamic_slice x15, local copies, waits for them, and re-layouts, combined_all(): lax.scan(lambda running, share: (join(running, share), None), head, tail)  13.5 us
    add x15, other arithmetic, merge_parts(): total_left * scale_left + total_right * scale_right  11.2 us
    unnamed x22, local copies, waits for them, and re-layouts  7.55 us
    all_to_all x1, starting transfers between devices, on_device(): lax.all_to_all(kv_cache, 'seq', split_axis=2, concat_axis=1, tiled=True)  7.44 us
  transfers between devices with their start and end apart: 3, of which 2 were waited for; matrix products, arithmetic and copies ran while one was open for 2% of the time, Pallas kernels for 0%

commit v1 on v0

--- a/solution.py
+++ b/solution.py
@@ -1,8 +1,11 @@
+import functools
 import math
 
 import jax
 import jax.numpy as jnp
 from jax import lax
+from jax.experimental import pallas as pl
+from jax.experimental.pallas import tpu as pltpu
 from jax.sharding import PartitionSpec as P
 
 H = 48
@@ -132,6 +135,496 @@
     return (attended, expert_out)
 
 
+def fused_kernel(
+    seq_count,
+    lengths,
+    routing,
+    residual,
+    queries,
+    new_entries,
+    kv_cache,
+    w_out,
+    gain,
+    router,
+    w_gate,
+    w_up,
+    w_down,
+    attended_out,
+    expert_out,
+    k_buf,
+    v_buf,
+    wo_buf,
+    gu_buf,
+    wd_buf,
+    router_buf,
+    gain_buf,
+    res_buf,
+    new_buf,
+    q_buf,
+    q_rows,
+    kn_rows,
+    vn_rows,
+    part_mine,
+    part_other,
+    attn_rows,
+    attn_buf,
+    proj_mine,
+    proj_other,
+    att_buf,
+    red_send,
+    red_buf,
+    load_sems,
+    q_sems,
+    part_sems,
+    attn_send,
+    attn_recv,
+    proj_sems,
+    att_send,
+    att_recv,
+    down_send,
+    down_recv,
+):
+    s = lax.axis_index("seq")
+    c = lax.axis_index("expert")
+    requests, width = residual.shape
+    per_group = H // KVH
+    rows = requests * per_group
+    columns = kv_cache.shape[2]
+    own_heads = KVH // 2
+    experts, features, hidden = w_gate.shape
+    owner_core = s // own_heads
+    slot = lax.rem(s, own_heads)
+    is_owner = c == owner_core
+    other = {"expert": 1 - c}
+    remote = functools.partial(
+        pltpu.make_async_remote_copy, device_id_type=pl.DeviceIdType.MESH
+    )
+
+    head_span = per_group * HD
+    q_cols = pl.ds(pl.multiple_of(slot * head_span, HD), head_span)
+    n_cols = pl.ds(pl.multiple_of(slot * HD, HD), HD)
+    load_q = pltpu.make_async_copy(queries.at[:, q_cols], q_buf, load_sems.at[0])
+    load_new = pltpu.make_async_copy(new_entries.at[:, :, n_cols], new_buf, load_sems.at[1])
+    load_k = pltpu.make_async_copy(kv_cache.at[0], k_buf, load_sems.at[2])
+    load_v = pltpu.make_async_copy(kv_cache.at[1], v_buf, load_sems.at[3])
+    load_wo = [
+        pltpu.make_async_copy(
+            w_out.at[pl.ds(h * head_span, head_span)], wo_buf.at[h], load_sems.at[4 + h]
+        )
+        for h in range(own_heads)
+    ]
+    at = 4 + own_heads
+    load_res = pltpu.make_async_copy(residual, res_buf, load_sems.at[at])
+    load_gain = pltpu.make_async_copy(gain, gain_buf, load_sems.at[at + 1])
+    load_router = pltpu.make_async_copy(router, router_buf, load_sems.at[at + 2])
+    load_gu = []
+    load_wd = []
+    for e in range(experts):
+        for i, w in enumerate((w_gate, w_up)):
+            load_gu.append(
+                pltpu.make_async_copy(
+                    w.at[e],
+                    gu_buf.at[:, pl.ds((2 * e + i) * hidden, hidden)],
+                    load_sems.at[at + 3],
+                )
+            )
+        load_wd.append(
+            pltpu.make_async_copy(
+                w_down.at[e], wd_buf.at[pl.ds(e * hidden, hidden)], load_sems.at[at + 4]
+            )
+        )
+
+    @pl.when(is_owner)
+    def _():
+        load_q.start()
+        load_new.start()
+
+    load_k.start()
+    load_v.start()
+    for load in load_wo:
+        load.start()
+    load_res.start()
+    load_gain.start()
+    load_router.start()
+    for load in load_gu + load_wd:
+        load.start()
+
+    barrier = pltpu.get_barrier_semaphore()
+    pl.semaphore_signal(barrier, inc=1, device_id=other, device_id_type=pl.DeviceIdType.MESH)
+    for step in range(1, seq_count):
+        peer = lax.rem(s + step, seq_count)
+        for core in range(2):
+            pl.semaphore_signal(
+                barrier,
+                inc=1,
+                device_id={"seq": peer, "expert": core},
+                device_id_type=pl.DeviceIdType.MESH,
+            )
+    pl.semaphore_wait(barrier, 2 * seq_count - 1)
+
+    send_q = remote(
+        src_ref=queries.at[:, q_cols],
+        dst_ref=q_buf,
+        send_sem=q_sems.at[0],
+        recv_sem=q_sems.at[1],
+        device_id=other,
+    )
+
+    @pl.when(is_owner)
+    def _():
+        send_q.start()
+        load_q.wait()
+        load_new.wait()
+
+    @pl.when(jnp.logical_not(is_owner))
+    def _():
+        send_q.wait_recv()
+
+    for t in range(per_group):
+        q_rows[pl.ds(t * requests, requests), :] = q_buf[:, pl.ds(t * HD, HD)].astype(jnp.float32)
+    q_f32 = q_rows[...]
+    scale = 1.0 / math.sqrt(HD)
+    load_k.wait()
+    scores = (
+        jnp.dot(q_f32.astype(jnp.bfloat16), k_buf[...], preferred_element_type=jnp.float32) * scale
+    )
+    row_id = lax.broadcasted_iota(jnp.int32, (rows, 1), 0)
+    row_req = lax.rem(row_id, requests)
+    limit = jnp.zeros((rows, 1), jnp.int32)
+    for r in range(requests):
+        limit = jnp.where(row_req == r, lengths[r], limit)
+    limit = limit * requests - c * columns
+    col_id = lax.broadcasted_iota(jnp.int32, (rows, columns), 1)
+    alive = ((col_id & (requests - 1)) == row_req) & (col_id < limit)
+    scores = jnp.where(alive, scores, -1e30)
+    highest = jnp.max(scores, axis=-1, keepdims=True)
+    weights = jnp.where(alive, jnp.exp(scores - highest), 0.0)
+    total = jnp.sum(weights, axis=-1, keepdims=True)
+    load_v.wait()
+    summed = lax.dot_general(
+        weights.astype(jnp.bfloat16),
+        v_buf[...],
+        (((1,), (1,)), ((), ())),
+        preferred_element_type=jnp.float32,
+    )
+
+    send_part = remote(
+        src_ref=part_mine,
+        dst_ref=part_other,
+        send_sem=part_sems.at[0],
+        recv_sem=part_sems.at[1],
+        device_id=other,
+    )
+    attn_copies = []
+    for step in range(1, seq_count):
+        peer = lax.rem(s + step, seq_count)
+        attn_copies.append(
+            remote(
+                src_ref=attn_buf.at[slot],
+                dst_ref=attn_buf.at[slot],
+                send_sem=attn_send,
+                recv_sem=attn_recv.at[slot],
+                device_id={"seq": peer},
+            )
+        )
+
+    lane = lax.broadcasted_iota(jnp.int32, (rows, HD), 1)
+
+    @pl.when(jnp.logical_not(is_owner))
+    def _():
+        part_mine[0] = summed
+        part_mine[1] = jnp.where(lane < HD // 2, highest, total)
+        send_part.start()
+
+    @pl.when(is_owner)
+    def _():
+        for t in range(per_group):
+            kn_rows[pl.ds(t * requests, requests), :] = new_buf[0].astype(jnp.float32)
+            vn_rows[pl.ds(t * requests, requests), :] = new_buf[1].astype(jnp.float32)
+        own = jnp.sum(q_f32 * kn_rows[...], axis=-1, keepdims=True) * scale
+        mine = jnp.maximum(highest, own)
+        send_part.wait_recv()
+        stats = part_other[1]
+        high_other = stats[:, 0:1]
+        total_other = stats[:, HD - 1 : HD]
+        joined = jnp.maximum(mine, high_other)
+        fade = jnp.exp(highest - joined)
+        fade_other = jnp.exp(high_other - joined)
+        own_weight = jnp.exp(own - joined)
+        numer = summed * fade + part_other[0] * fade_other + own_weight * vn_rows[...]
+        denom = total * fade + total_other * fade_other + own_weight
+        attn_rows[...] = numer / denom
+        for t in range(per_group):
+            attn_buf[slot, :, pl.ds(t * HD, HD)] = attn_rows[
+                pl.ds(t * requests, requests), :
+            ].astype(jnp.bfloat16)
+        for copy in attn_copies:
+            copy.start()
+
+    proj = jnp.zeros((requests, width), jnp.float32)
+    for h in range(own_heads):
+        load_wo[h].wait()
+
+        @pl.when(jnp.logical_not(is_owner & (slot == h)))
+        def _():
+            remote(
+                src_ref=attn_buf.at[h],
+                dst_ref=attn_buf.at[h],
+                send_sem=attn_send,
+                recv_sem=attn_recv.at[h],
+                device_id=other,
+            ).wait_recv()
+
+        proj = proj + jnp.dot(attn_buf[h], wo_buf[h], preferred_element_type=jnp.float32)
+    proj_mine[...] = proj
+    send_proj = remote(
+        src_ref=proj_mine,
+        dst_ref=proj_other,
+        send_sem=proj_sems.at[0],
+        recv_sem=proj_sems.at[1],
+        device_id=other,
+    )
+    send_proj.start()
+    load_res.wait()
+    load_gain.wait()
+    load_router.wait()
+    for load in load_gu:
+        load.wait()
+    res_f32 = res_buf[...].astype(jnp.float32)
+    send_proj.wait_recv()
+    attended = (res_f32 + (proj + proj_other[...])).astype(jnp.bfloat16)
+    att_buf[s] = attended
+    attended_out[...] = attended
+    att_copies = []
+    for step in range(1, seq_count):
+        peer = lax.rem(s + step, seq_count)
+        att_copies.append(
+            remote(
+                src_ref=att_buf.at[s],
+                dst_ref=att_buf.at[s],
+                send_sem=att_send,
+                recv_sem=att_recv.at[s],
+                device_id={"seq": peer},
+            )
+        )
+    for copy in att_copies:
+        copy.start()
+
+    squares = jnp.zeros((requests, 1), jnp.float32)
+    logits = jnp.zeros((requests, router.shape[0]), jnp.float32)
+    gu = jnp.zeros((requests, 2 * experts * hidden), jnp.float32)
+    for i in range(seq_count):
+
+        @pl.when(s != i)
+        def _():
+            remote(
+                src_ref=att_buf.at[i],
+                dst_ref=att_buf.at[i],
+                send_sem=att_send,
+                recv_sem=att_recv.at[i],
+                device_id=other,
+            ).wait_recv()
+
+        x = att_buf[i].astype(jnp.float32)
+        squares = squares + jnp.sum(x * x, axis=-1, keepdims=True)
+        scaled = (x * gain_buf[:, pl.ds(i * width, width)]).astype(jnp.bfloat16)
+        logits = logits + lax.dot_general(
+            scaled,
+            router_buf[:, pl.ds(i * width, width)],
+            (((1,), (1,)), ((), ())),
+            preferred_element_type=jnp.float32,
+        )
+        gu = gu + jnp.dot(
+            scaled, gu_buf[pl.ds(i * width, width), :], preferred_element_type=jnp.float32
+        )
+    inverse = lax.rsqrt(squares * (1.0 / features) + 1e-05)
+    logits = logits * inverse
+    gu = gu * inverse
+    req_id = lax.broadcasted_iota(jnp.int32, (requests, 1), 0)
+    first_id = jnp.zeros((requests, 1), jnp.int32)
+    second_id = jnp.zeros((requests, 1), jnp.int32)
+    for r in range(requests):
+        first_id = jnp.where(req_id == r, routing[0, r], first_id)
+        second_id = jnp.where(req_id == r, routing[1, r], second_id)
+    expert_id = lax.broadcasted_iota(jnp.int32, logits.shape, 1)
+    gap = jnp.sum(
+        jnp.where(expert_id == first_id, logits, 0.0)
+        - jnp.where(expert_id == second_id, logits, 0.0),
+        axis=-1,
+        keepdims=True,
+    )
+    first_share = 1.0 / (1.0 + jnp.exp(-gap))
+    acts = []
+    for e in range(experts):
+        number = c * experts + e
+        share = jnp.where(number == first_id, first_share, 0.0) + jnp.where(
+            number == second_id, 1.0 - first_share, 0.0
+        )
+        gate = gu[:, 2 * e * hidden : (2 * e + 1) * hidden]
+        up = gu[:, (2 * e + 1) * hidden : (2 * e + 2) * hidden]
+        acts.append((gate / (1.0 + jnp.exp(-gate)) * up * share).astype(jnp.bfloat16))
+    act = jnp.concatenate(acts, axis=1)
+    for load in load_wd:
+        load.wait()
+
+    me = s * 2 + c
+    down_copies = []
+    for step in range(1, seq_count + 1):
+        peer = lax.rem(s + step, seq_count)
+        block = jnp.dot(
+            act,
+            wd_buf[:, pl.ds(pl.multiple_of(peer * width, HD), width)],
+            preferred_element_type=jnp.float32,
+        ).astype(jnp.bfloat16)
+        if step < seq_count:
+            red_send[step - 1] = block
+            for core in range(2):
+                copy = remote(
+                    src_ref=red_send.at[step - 1],
+                    dst_ref=red_buf.at[me],
+                    send_sem=down_send,
+                    recv_sem=down_recv.at[me],
+                    device_id={"seq": peer, "expert": core},
+                )
+                copy.start()
+                down_copies.append(copy)
+        else:
+            red_buf[me] = block
+            copy = remote(
+                src_ref=red_buf.at[me],
+                dst_ref=red_buf.at[me],
+                send_sem=down_send,
+                recv_sem=down_recv.at[me],
+                device_id=other,
+            )
+            copy.start()
+            down_copies.append(copy)
+    result = jnp.zeros((requests, width), jnp.float32)
+    for i in range(2 * seq_count):
+
+        @pl.when(me != i)
+        def _():
+            remote(
+                src_ref=red_buf.at[i],
+                dst_ref=red_buf.at[i],
+                send_sem=down_send,
+                recv_sem=down_recv.at[i],
+                device_id=other,
+            ).wait_recv()
+
+        result = result + red_buf[i].astype(jnp.float32)
+    expert_out[...] = result.astype(jnp.bfloat16)
+
+    @pl.when(is_owner)
+    def _():
+        send_q.wait_send()
+        for copy in attn_copies:
+            copy.wait_send()
+
+    @pl.when(jnp.logical_not(is_owner))
+    def _():
+        send_part.wait_send()
+
+    send_proj.wait_send()
+    for copy in att_copies + down_copies:
+        copy.wait_send()
+
+
+def fused_step(
+    residual,
+    queries,
+    new_entries,
+    kv_cache,
+    lengths,
+    routing,
+    w_out,
+    norm_gain,
+    router,
+    w_gate,
+    w_up,
+    w_down,
+):
+    seq_count = lax.axis_size("seq")
+    requests, width = residual.shape
+    per_group = H // KVH
+    own_heads = KVH // 2
+    rows = requests * per_group
+    columns = kv_cache.shape[2]
+    experts, features, hidden = w_gate.shape
+    gain = norm_gain.astype(jnp.float32).reshape(1, features)
+    bf16, f32 = jnp.bfloat16, jnp.float32
+    vmem = pltpu.VMEM
+    dma = pltpu.SemaphoreType.DMA
+    anywhere = pl.BlockSpec(memory_space=pl.ANY)
+    out = jax.ShapeDtypeStruct((requests, width), bf16)
+    return pl.pallas_call(
+        functools.partial(fused_kernel, seq_count),
+        out_shape=(out, out),
+        in_specs=[pl.BlockSpec(memory_space=pltpu.SMEM)] * 2 + [anywhere] * 10,
+        out_specs=(pl.BlockSpec(memory_space=vmem),) * 2,
+        scratch_shapes=[
+            vmem((HD, columns), bf16),
+            vmem((HD, columns), bf16),
+            vmem((own_heads, per_group * HD, width), bf16),
+            vmem((features, 2 * experts * hidden), bf16),
+            vmem((experts * hidden, features), bf16),
+            vmem((router.shape[1], features), bf16),
+            vmem((1, features), f32),
+            vmem((requests, width), bf16),
+            vmem((2, requests, HD), bf16),
+            vmem((requests, per_group * HD), bf16),
+            vmem((rows, HD), f32),
+            vmem((rows, HD), f32),
+            vmem((rows, HD), f32),
+            vmem((2, rows, HD), f32),
+            vmem((2, rows, HD), f32),
+            vmem((rows, HD), f32),
+            vmem((own_heads, requests, per_group * HD), bf16),
+            vmem((requests, width), f32),
+            vmem((requests, width), f32),
+            vmem((seq_count, requests, width), bf16),
+            vmem((seq_count, requests, width), bf16),
+            vmem((2 * seq_count, requests, width), bf16),
+            dma((9 + own_heads,)),
+            dma((2,)),
+            dma((2,)),
+            dma,
+            dma((own_heads,)),
+            dma((2,)),
+            dma,
+            dma((seq_count,)),
+            dma,
+            dma((2 * seq_count,)),
+        ],
+        compiler_params=pltpu.CompilerParams(
+            collective_id=0, has_side_effects=True, vmem_limit_bytes=60 * 1024 * 1024
+        ),
+        name="decode_step",
+    )(
+        lengths,
+        routing.T,
+        residual,
+        queries,
+        new_entries,
+        kv_cache,
+        w_out,
+        gain,
+        router.T,
+        w_gate,
+        w_up,
+        w_down,
+    )
+
+
+def step_on_device(*args):
+    kv_cache, lengths = args[3], args[4]
+    requests = lengths.shape[0]
+    whole_head = kv_cache.shape[1] == HD and lax.axis_size("seq") == KVH
+    if whole_head and lax.axis_size("expert") == 2 and requests & (requests - 1) == 0:
+        return fused_step(*args)
+    return on_device(*args)
+
+
 def solution(mesh):
     in_specs = (
         P("groups", "seq"),
@@ -149,5 +642,5 @@
     )
     out_specs = (P("groups", "seq"), P("groups", "seq"))
     return jax.shard_map(
-        on_device, mesh=mesh, in_specs=in_specs, out_specs=out_specs, check_vma=False
-    )
+        step_on_device, mesh=mesh, in_specs=in_specs, out_specs=out_specs, check_vma=False
+    )

time: 288 us -> 31 us (0.11)
  waiting for transfers between devices: 119 us -> 0 us
  blocking collectives: 78.8 us -> 0 us
  local copies, waits for them, and re-layouts: 35.9 us -> 2.58 us
  Pallas kernels: 0 us -> 26.1 us
  other arithmetic: 16.7 us -> 1.31 us
  between operations: 14.3 us -> 0.64 us
  matrix products: 13.4 us -> 0 us
  starting transfers between devices: 7.52 us -> 0 us
    unnamed x3 -> x0, waiting for transfers between devices: 72.9 us -> none
    all_gather x4 -> x0, blocking collectives: 71.5 us -> none  [the longest x2 38.9 us: combined_all(): pieces = jax.tree.map(lambda part: lax.all_gather(part, axis), value)]
    all_to_all x1 -> x0, waiting for transfers between devices: 46.3 us -> none  [on_device(): lax.all_to_all(kv_cache, 'seq', split_axis=2, concat_axis=1, tiled=True)]
    pallas_call x0 -> x1, Pallas kernels: none -> 26.1 us  [fused_step(): pl.pallas_call(functools.partial(fused_kernel, seq_count), out_shape=(out...]
    add x33 -> x0, other arithmetic: 14.3 us -> none  [the longest x15 11.2 us: merge_parts(): total_left * scale_left + total_right * scale_right]
    dynamic_slice x15 -> x0, local copies, waits for them, and re-layouts: 13.5 us -> none  [combined_all(): lax.scan(lambda running, share: (join(running, share), None), head, tail)]
    dot_general x7 -> x0, matrix products: 13.4 us -> none  [the longest x1 5.85 us: on_device(): jnp.einsum('ref,efd->rd', activation, w_down, preferred_element_type=jnp....]
    all_to_all x1 -> x0, starting transfers between devices: 7.44 us -> none  [on_device(): lax.all_to_all(kv_cache, 'seq', split_axis=2, concat_axis=1, tiled=True)]
  transfers between devices with their start and end apart: 3 -> 0, of which waited for: 2 -> 0; matrix products, arithmetic and copies ran while one was open for 2% -> 0% of each run, Pallas kernels for 0% -> 0%
where the time goes in v1:
time: 31 us; the launch traced here: 30.6 us
  Pallas kernels  26.1 us (84%)
  local copies, waits for them, and re-layouts  2.58 us (8%)
  other arithmetic  1.31 us (4%)
  between operations  0.64 us (2%)
    pallas_call x1, Pallas kernels, fused_step(): pl.pallas_call(functools.partial(fused_kernel, seq_count), out_shape=(out...  26.1 us
    unnamed x2, local copies, waits for them, and re-layouts  2.58 us
    reshape x1, other arithmetic, fused_step(): gain = norm_gain.astype(jnp.float32).reshape(1, features)  1.31 us

profile of v1, /device:TPU:0, one launch (start us, length us, event | category | flops | bytes accessed | tf_op | source)
XLA Modules:
  0.0 30.6 jit_solution(537445241400953830)
XLA Ops:
  0.6 1.3 %reshape.11 = f32[6144]{0:T(1024)} convert(bf16[6144]{0:T(1024)(128)(2,1)} %param.19) | non-fusion elementwise | flops 6144 | bytes 36864 | tf_op jit(solution)/shard_map/reshape | solution.py:554
  1.9 26.1 %decode_step.1 = (bf16[4,768]{1,0:T(4,128)(2,1)}, bf16[4,768]{1,0:T(4,128)(2,1)}) custom-call(s32[4]{0:T(128)} %lengths.1, s32[2,4]{1,0:T(2,128)} %bitcast.5, bf16[4,768]{1,0:T(4,128)(2,1)} %residual.1, bf16[4,3072]{1,0:T(4,128)(2,1)} %queries.1, bf16[2,4,512]{2,1,0:T(4,128)(2,1)} %new_entries.1, bf16[2,128,4096]{2,1,0:T(8,128)(2,1)} %kv_cache.1, ...), custom_call_target="tpu_custom_call" | custom-call | tf_op jit(solution)/shard_map/decode_step/pallas_call | solution.py:560
  28.0 1.3 %copy.16 = bf16[4,768]{1,0:T(4,128)(2,1)} copy(bf16[4,768]{1,0:T(4,128)(2,1)} %get-tuple-element.4) | data formatting | bytes 12288
  29.3 1.3 %copy.17 = bf16[4,768]{1,0:T(4,128)(2,1)} copy(bf16[4,768]{1,0:T(4,128)(2,1)} %get-tuple-element.5) | data formatting | bytes 12288

commit v2 on v1

--- a/solution.py
+++ b/solution.py
@@ -149,8 +149,7 @@
     w_gate,
     w_up,
     w_down,
-    attended_out,
-    expert_out,
+    outs,
     k_buf,
     v_buf,
     wo_buf,
@@ -394,7 +393,7 @@
     send_proj.wait_recv()
     attended = (res_f32 + (proj + proj_other[...])).astype(jnp.bfloat16)
     att_buf[s] = attended
-    attended_out[...] = attended
+    outs[0] = attended
     att_copies = []
     for step in range(1, seq_count):
         peer = lax.rem(s + step, seq_count)
@@ -427,7 +426,7 @@
 
         x = att_buf[i].astype(jnp.float32)
         squares = squares + jnp.sum(x * x, axis=-1, keepdims=True)
-        scaled = (x * gain_buf[:, pl.ds(i * width, width)]).astype(jnp.bfloat16)
+        scaled = (x * gain_buf[pl.ds(i * width, width)].astype(jnp.float32)[None, :]).astype(jnp.bfloat16)
         logits = logits + lax.dot_general(
             scaled,
             router_buf[:, pl.ds(i * width, width)],
@@ -513,7 +512,7 @@
             ).wait_recv()
 
         result = result + red_buf[i].astype(jnp.float32)
-    expert_out[...] = result.astype(jnp.bfloat16)
+    outs[1] = result.astype(jnp.bfloat16)
 
     @pl.when(is_owner)
     def _():
@@ -551,17 +550,16 @@
     rows = requests * per_group
     columns = kv_cache.shape[2]
     experts, features, hidden = w_gate.shape
-    gain = norm_gain.astype(jnp.float32).reshape(1, features)
     bf16, f32 = jnp.bfloat16, jnp.float32
     vmem = pltpu.VMEM
     dma = pltpu.SemaphoreType.DMA
     anywhere = pl.BlockSpec(memory_space=pl.ANY)
-    out = jax.ShapeDtypeStruct((requests, width), bf16)
-    return pl.pallas_call(
+    out = jax.ShapeDtypeStruct((2, requests, width), bf16)
+    outs = pl.pallas_call(
         functools.partial(fused_kernel, seq_count),
-        out_shape=(out, out),
+        out_shape=out,
         in_specs=[pl.BlockSpec(memory_space=pltpu.SMEM)] * 2 + [anywhere] * 10,
-        out_specs=(pl.BlockSpec(memory_space=vmem),) * 2,
+        out_specs=pl.BlockSpec(memory_space=vmem),
         scratch_shapes=[
             vmem((HD, columns), bf16),
             vmem((HD, columns), bf16),
@@ -569,7 +567,7 @@
             vmem((features, 2 * experts * hidden), bf16),
             vmem((experts * hidden, features), bf16),
             vmem((router.shape[1], features), bf16),
-            vmem((1, features), f32),
+            vmem((features,), bf16),
             vmem((requests, width), bf16),
             vmem((2, requests, HD), bf16),
             vmem((requests, per_group * HD), bf16),
@@ -608,12 +606,13 @@
         new_entries,
         kv_cache,
         w_out,
-        gain,
+        norm_gain,
         router.T,
         w_gate,
         w_up,
         w_down,
     )
+    return (outs[0], outs[1])
 
 
 def step_on_device(*args):

time: 31 us -> 28.3 us (0.913)
  other arithmetic: 1.31 us -> 0 us
  local copies, waits for them, and re-layouts: 2.58 us -> 1.31 us
    unnamed x2 -> x0, local copies, waits for them, and re-layouts: 2.58 us -> none
    reshape x1 -> x0, other arithmetic: 1.31 us -> none  [fused_step(): gain = norm_gain.astype(jnp.float32).reshape(1, features)]
    squeeze x0 -> x1, local copies, waits for them, and re-layouts: none -> 1.31 us  [fused_step(): return (outs[0], outs[1])]
where the time goes in v2:
time: 28.3 us; the launch traced here: 28.1 us
  Pallas kernels  26.1 us (92%)
  local copies, waits for them, and re-layouts  1.31 us (5%)
  between operations  0.64 us (2%)
    pallas_call x1, Pallas kernels, fused_step(): pl.pallas_call(functools.partial(fused_kernel, seq_count), out_shape=out,...  26.1 us
    squeeze x1, local copies, waits for them, and re-layouts, fused_step(): return (outs[0], outs[1])  1.31 us

profile of v2, /device:TPU:0, one launch (start us, length us, event | category | flops | bytes accessed | tf_op | source)
XLA Modules:
  0.0 28.1 jit_solution(15901018246870708492)
XLA Ops:
  0.6 26.1 %decode_step.1 = bf16[2,4,768]{2,1,0:T(4,128)(2,1)} custom-call(s32[4]{0:T(128)} %lengths.1, s32[2,4]{1,0:T(2,128)} %bitcast.7, bf16[4,768]{1,0:T(4,128)(2,1)} %residual.1, bf16[4,3072]{1,0:T(4,128)(2,1)} %queries.1, bf16[2,4,512]{2,1,0:T(4,128)(2,1)} %new_entries.1, bf16[2,128,4096]{2,1,0:T(8,128)(2,1)} %kv_cache.1, bf16[3072,768]{1,0:T(8,128)(2,1)} %w_out.1, ...), custom_call_target="tpu_custom_call" | custom-call | tf_op jit(solution)/shard_map/decode_step/pallas_call | solution.py:558
  26.8 1.3 %slice_bitcast_fusion = (bf16[4,768]{1,0:T(4,128)(2,1)}, bf16[4,768]{1,0:T(4,128)(2,1)}) fusion(bf16[2,4,768]{2,1,0:T(4,128)(2,1)} %decode_step.1), kind=kLoop, calls=%fused_computation | loop fusion | bytes 24576 | tf_op jit(solution)/shard_map/squeeze | solution.py:615

commit v3 on v2

--- a/solution.py
+++ b/solution.py
@@ -137,8 +137,8 @@
 
 def fused_kernel(
     seq_count,
-    lengths,
-    routing,
+    lengths_in,
+    routing_in,
     residual,
     queries,
     new_entries,
@@ -172,6 +172,8 @@
     att_buf,
     red_send,
     red_buf,
+    lengths,
+    routing,
     load_sems,
     q_sems,
     part_sems,
@@ -238,6 +240,10 @@
         load_q.start()
         load_new.start()
 
+    load_lengths = pltpu.make_async_copy(lengths_in, lengths, load_sems.at[at + 5])
+    load_routing = pltpu.make_async_copy(routing_in, routing, load_sems.at[at + 6])
+    load_lengths.start()
+    load_routing.start()
     load_k.start()
     load_v.start()
     for load in load_wo:
@@ -284,6 +290,8 @@
     q_f32 = q_rows[...]
     scale = 1.0 / math.sqrt(HD)
     load_k.wait()
+    load_lengths.wait()
+    load_routing.wait()
     scores = (
         jnp.dot(q_f32.astype(jnp.bfloat16), k_buf[...], preferred_element_type=jnp.float32) * scale
     )
@@ -360,7 +368,6 @@
         for copy in attn_copies:
             copy.start()
 
-    proj = jnp.zeros((requests, width), jnp.float32)
     for h in range(own_heads):
         load_wo[h].wait()
 
@@ -374,7 +381,11 @@
                 device_id=other,
             ).wait_recv()
 
-        proj = proj + jnp.dot(attn_buf[h], wo_buf[h], preferred_element_type=jnp.float32)
+    proj = jnp.dot(
+        jnp.concatenate([attn_buf[h] for h in range(own_heads)], axis=1),
+        wo_buf[...].reshape(own_heads * head_span, width),
+        preferred_element_type=jnp.float32,
+    )
     proj_mine[...] = proj
     send_proj = remote(
         src_ref=proj_mine,
@@ -409,9 +420,6 @@
     for copy in att_copies:
         copy.start()
 
-    squares = jnp.zeros((requests, 1), jnp.float32)
-    logits = jnp.zeros((requests, router.shape[0]), jnp.float32)
-    gu = jnp.zeros((requests, 2 * experts * hidden), jnp.float32)
     for i in range(seq_count):
 
         @pl.when(s != i)
@@ -424,18 +432,13 @@
                 device_id=other,
             ).wait_recv()
 
-        x = att_buf[i].astype(jnp.float32)
-        squares = squares + jnp.sum(x * x, axis=-1, keepdims=True)
-        scaled = (x * gain_buf[pl.ds(i * width, width)].astype(jnp.float32)[None, :]).astype(jnp.bfloat16)
-        logits = logits + lax.dot_general(
-            scaled,
-            router_buf[:, pl.ds(i * width, width)],
-            (((1,), (1,)), ((), ())),
-            preferred_element_type=jnp.float32,
-        )
-        gu = gu + jnp.dot(
-            scaled, gu_buf[pl.ds(i * width, width), :], preferred_element_type=jnp.float32
-        )
+    x = jnp.concatenate([att_buf[i] for i in range(seq_count)], axis=1).astype(jnp.float32)
+    scaled = (x * gain_buf[...].astype(jnp.float32)[None, :]).astype(jnp.bfloat16)
+    gu = jnp.dot(scaled, gu_buf[...], preferred_element_type=jnp.float32)
+    squares = jnp.sum(x * x, axis=-1, keepdims=True)
+    logits = lax.dot_general(
+        scaled, router_buf[...], (((1,), (1,)), ((), ())), preferred_element_type=jnp.float32
+    )
     inverse = lax.rsqrt(squares * (1.0 / features) + 1e-05)
     logits = logits * inverse
     gu = gu * inverse
@@ -468,37 +471,37 @@
 
     me = s * 2 + c
     down_copies = []
-    for step in range(1, seq_count + 1):
-        peer = lax.rem(s + step, seq_count)
-        block = jnp.dot(
-            act,
-            wd_buf[:, pl.ds(pl.multiple_of(peer * width, HD), width)],
-            preferred_element_type=jnp.float32,
-        ).astype(jnp.bfloat16)
-        if step < seq_count:
-            red_send[step - 1] = block
+    steps = sorted(range(seq_count), key=lambda step: -min(step, seq_count - step))
+    half = seq_count // 2
+    for group in (steps[:half], steps[half:]):
+        blocks = []
+        for step in group:
+            peer = lax.rem(s + step, seq_count)
+            block = jnp.dot(
+                act,
+                wd_buf[:, pl.ds(pl.multiple_of(peer * width, HD), width)],
+                preferred_element_type=jnp.float32,
+            )
+            blocks.append(block.astype(jnp.bfloat16))
+        for step, block in zip(group, blocks):
+            if step:
+                red_send[step - 1] = block
+            else:
+                red_buf[me] = block
+        for step in group:
+            peer = lax.rem(s + step, seq_count)
             for core in range(2):
-                copy = remote(
-                    src_ref=red_send.at[step - 1],
-                    dst_ref=red_buf.at[me],
-                    send_sem=down_send,
-                    recv_sem=down_recv.at[me],
-                    device_id={"seq": peer, "expert": core},
-                )
-                copy.start()
-                down_copies.append(copy)
-        else:
-            red_buf[me] = block
-            copy = remote(
-                src_ref=red_buf.at[me],
-                dst_ref=red_buf.at[me],
-                send_sem=down_send,
-                recv_sem=down_recv.at[me],
-                device_id=other,
-            )
-            copy.start()
-            down_copies.append(copy)
-    result = jnp.zeros((requests, width), jnp.float32)
+                target = {"seq": peer, "expert": core} if step else other
+                if step or core:
+                    copy = remote(
+                        src_ref=red_send.at[step - 1] if step else red_buf.at[me],
+                        dst_ref=red_buf.at[me],
+                        send_sem=down_send,
+                        recv_sem=down_recv.at[me],
+                        device_id=target,
+                    )
+                    copy.start()
+                    down_copies.append(copy)
     for i in range(2 * seq_count):
 
         @pl.when(me != i)
@@ -511,7 +514,7 @@
                 device_id=other,
             ).wait_recv()
 
-        result = result + red_buf[i].astype(jnp.float32)
+    result = jnp.sum(red_buf[...].astype(jnp.float32), axis=0)
     outs[1] = result.astype(jnp.bfloat16)
 
     @pl.when(is_owner)
@@ -553,12 +556,11 @@
     bf16, f32 = jnp.bfloat16, jnp.float32
     vmem = pltpu.VMEM
     dma = pltpu.SemaphoreType.DMA
-    anywhere = pl.BlockSpec(memory_space=pl.ANY)
-    out = jax.ShapeDtypeStruct((2, requests, width), bf16)
+    anywhere = pl.BlockSpec(memory_space=pltpu.HBM)
     outs = pl.pallas_call(
         functools.partial(fused_kernel, seq_count),
-        out_shape=out,
-        in_specs=[pl.BlockSpec(memory_space=pltpu.SMEM)] * 2 + [anywhere] * 10,
+        out_shape=pltpu.VMEM((2, requests, width), bf16),
+        in_specs=[anywhere] * 12,
         out_specs=pl.BlockSpec(memory_space=vmem),
         scratch_shapes=[
             vmem((HD, columns), bf16),
@@ -583,7 +585,9 @@
             vmem((seq_count, requests, width), bf16),
             vmem((seq_count, requests, width), bf16),
             vmem((2 * seq_count, requests, width), bf16),
-            dma((9 + own_heads,)),
+            pltpu.SMEM((requests,), jnp.int32),
+            pltpu.SMEM((2, requests), jnp.int32),
+            dma((11 + own_heads,)),
             dma((2,)),
             dma((2,)),
             dma,

time: 28.3 us -> 25.9 us (0.915)
  Pallas kernels: 26.1 us -> 24.5 us
  local copies, waits for them, and re-layouts: 1.31 us -> 0.6 us
    pallas_call x1, Pallas kernels: 26.1 us -> 24.5 us  [fused_step(): pl.pallas_call(functools.partial(fused_kernel, seq_count), out_shape=pltp...]
    squeeze x1, local copies, waits for them, and re-layouts: 1.31 us -> 0.6 us  [fused_step(): return (outs[0], outs[1])]
where the time goes in v3:
time: 25.9 us; the launch traced here: 25.7 us
  Pallas kernels  24.5 us (95%)
  between operations  0.64 us (2%)
  local copies, waits for them, and re-layouts  0.6 us (2%)
    pallas_call x1, Pallas kernels, fused_step(): pl.pallas_call(functools.partial(fused_kernel, seq_count), out_shape=pltp...  24.5 us
    squeeze x1, local copies, waits for them, and re-layouts, fused_step(): return (outs[0], outs[1])  0.6 us

profile of v3, /device:TPU:0, one launch (start us, length us, event | category | flops | bytes accessed | tf_op | source)
XLA Modules:
  0.0 25.7 jit_solution(15474538646687258135)
XLA Ops:
  0.6 24.5 %decode_step.1 = bf16[2,4,768]{2,1,0:T(4,128)(2,1)S(1)} custom-call(s32[4]{0:T(128)} %lengths_in.1, s32[2,4]{1,0:T(2,128)} %bitcast.7, bf16[4,768]{1,0:T(4,128)(2,1)} %residual.1, bf16[4,3072]{1,0:T(4,128)(2,1)} %queries.1, bf16[2,4,512]{2,1,0:T(4,128)(2,1)} %new_entries.1, bf16[2,128,4096]{2,1,0:T(8,128)(2,1)} %kv_cache.1, bf16[3072,768]{1,0:T(8,128)(2,1)} %w_out.1, ...), custom_call_target="tpu_custom_call" | custom-call | tf_op jit(solution)/shard_map/decode_step/pallas_call | solution.py:560
  25.1 0.6 %slice_bitcast_fusion = (bf16[4,768]{1,0:T(4,128)(2,1)}, bf16[4,768]{1,0:T(4,128)(2,1)}) fusion(bf16[2,4,768]{2,1,0:T(4,128)(2,1)S(1)} %decode_step.1), kind=kLoop, calls=%fused_computation | loop fusion | bytes 24576 | tf_op jit(solution)/shard_map/squeeze | solution.py:619

commit v4 on v3

--- a/solution.py
+++ b/solution.py
@@ -172,6 +172,7 @@
     att_buf,
     red_send,
     red_buf,
+    relay_sems,
     lengths,
     routing,
     load_sems,
@@ -254,18 +255,33 @@
     for load in load_gu + load_wd:
         load.start()
 
+    has_up = s + 2 < seq_count
+    has_down = s >= 2
+    signal = functools.partial(pl.semaphore_signal, inc=1, device_id_type=pl.DeviceIdType.MESH)
+
+    def tell_neighbours(sem):
+        signal(sem, device_id={"seq": s ^ 1})
+
+        @pl.when(has_up)
+        def _():
+            signal(sem, device_id={"seq": s + 2})
+
+        @pl.when(has_down)
+        def _():
+            signal(sem, device_id={"seq": s - 2})
+
+    neighbours = 1 + has_up.astype(jnp.int32) + has_down.astype(jnp.int32)
     barrier = pltpu.get_barrier_semaphore()
-    pl.semaphore_signal(barrier, inc=1, device_id=other, device_id_type=pl.DeviceIdType.MESH)
-    for step in range(1, seq_count):
-        peer = lax.rem(s + step, seq_count)
-        for core in range(2):
-            pl.semaphore_signal(
-                barrier,
-                inc=1,
-                device_id={"seq": peer, "expert": core},
-                device_id_type=pl.DeviceIdType.MESH,
-            )
-    pl.semaphore_wait(barrier, 2 * seq_count - 1)
+    signal(barrier, device_id=other)
+    tell_neighbours(barrier)
+    pl.semaphore_wait(barrier, neighbours + 1)
+    relays = seq_count // 2 - 1
+    tell_neighbours(relay_sems.at[0])
+
+    def relay(i):
+        pl.semaphore_wait(relay_sems.at[i], neighbours)
+        if i + 1 < relays:
+            tell_neighbours(relay_sems.at[i + 1])
 
     send_q = remote(
         src_ref=queries.at[:, q_cols],
@@ -288,6 +304,7 @@
     for t in range(per_group):
         q_rows[pl.ds(t * requests, requests), :] = q_buf[:, pl.ds(t * HD, HD)].astype(jnp.float32)
     q_f32 = q_rows[...]
+    relay(0)
     scale = 1.0 / math.sqrt(HD)
     load_k.wait()
     load_lengths.wait()
@@ -308,6 +325,7 @@
     weights = jnp.where(alive, jnp.exp(scores - highest), 0.0)
     total = jnp.sum(weights, axis=-1, keepdims=True)
     load_v.wait()
+    relay(1)
     summed = lax.dot_general(
         weights.astype(jnp.bfloat16),
         v_buf[...],
@@ -342,6 +360,8 @@
         part_mine[0] = summed
         part_mine[1] = jnp.where(lane < HD // 2, highest, total)
         send_part.start()
+        for i in range(2, relays):
+            relay(i)
 
     @pl.when(is_owner)
     def _():
@@ -365,6 +385,8 @@
             attn_buf[slot, :, pl.ds(t * HD, HD)] = attn_rows[
                 pl.ds(t * requests, requests), :
             ].astype(jnp.bfloat16)
+        for i in range(2, relays):
+            relay(i)
         for copy in attn_copies:
             copy.start()
 
@@ -585,6 +607,7 @@
             vmem((seq_count, requests, width), bf16),
             vmem((seq_count, requests, width), bf16),
             vmem((2 * seq_count, requests, width), bf16),
+            pltpu.SemaphoreType.REGULAR((seq_count // 2 - 1,)),
             pltpu.SMEM((requests,), jnp.int32),
             pltpu.SMEM((2, requests), jnp.int32),
             dma((11 + own_heads,)),

time: 25.9 us -> 25.7 us (level)
  no operation moved by 1% of the time
where the time goes in v4:
time: 25.7 us; the launch traced here: 25.5 us
  Pallas kernels  24.3 us (95%)
  between operations  0.64 us (2%)
  local copies, waits for them, and re-layouts  0.6 us (2%)
    pallas_call x1, Pallas kernels, fused_step(): pl.pallas_call(functools.partial(fused_kernel, seq_count), out_shape=pltp...  24.3 us
    squeeze x1, local copies, waits for them, and re-layouts, fused_step(): return (outs[0], outs[1])  0.6 us

profile of v4, /device:TPU:0, one launch (start us, length us, event | category | flops | bytes accessed | tf_op | source)
XLA Modules:
  0.0 25.5 jit_solution(3168625501763284223)
XLA Ops:
  0.6 24.3 %decode_step.1 = bf16[2,4,768]{2,1,0:T(4,128)(2,1)S(1)} custom-call(s32[4]{0:T(128)} %lengths_in.1, s32[2,4]{1,0:T(2,128)} %bitcast.7, bf16[4,768]{1,0:T(4,128)(2,1)} %residual.1, bf16[4,3072]{1,0:T(4,128)(2,1)} %queries.1, bf16[2,4,512]{2,1,0:T(4,128)(2,1)} %new_entries.1, bf16[2,128,4096]{2,1,0:T(8,128)(2,1)} %kv_cache.1, bf16[3072,768]{1,0:T(8,128)(2,1)} %w_out.1, ...), custom_call_target="tpu_custom_call" | custom-call | tf_op jit(solution)/shard_map/decode_step/pallas_call | solution.py:582
  24.9 0.6 %slice_bitcast_fusion = (bf16[4,768]{1,0:T(4,128)(2,1)}, bf16[4,768]{1,0:T(4,128)(2,1)}) fusion(bf16[2,4,768]{2,1,0:T(4,128)(2,1)S(1)} %decode_step.1), kind=kLoop, calls=%fused_computation | loop fusion | bytes 24576 | tf_op jit(solution)/shard_map/squeeze | solution.py:642
